TPU v7x, 32 devices: a whole 2x2x4 slice. The times are simulated.
32 devices in a mesh: tp: 8 (over z, y), kv: 4 (over x, core).
Axes of the slice: x: 2, y: 2, z: 4, core: 2. Of those that a mesh axis runs over, the one named last changes fastest.
Arguments:
- hidden_in: bfloat16 [2048, 4096], P(('kv', 'tp')), may hold values from -6 to 6
- gain_attn: float32 [4096], replicated, may hold values from 0.4 to 1.6
- w_qkv: bfloat16 [4096, 32, 384], P(None, 'tp'), may hold values from -0.09375 to 0.09375
- cache_kv: bfloat16 [2, 8192, 32, 256], P(None, 'kv', 'tp'), may hold values from -110 to 110
- cache_len: int32 [2], replicated, may hold values from 128 to 8192, as said below
- w_out: bfloat16 [4096, 4096], P('tp'), may hold values from -0.1875 to 0.1875
- gain_mlp: float32 [4096], replicated, may hold values from 0.1 to 1.9
- w_gate_up: bfloat16 [4096, 2, 11008], P('kv', None, 'tp'), may hold values from -0.09375 to 0.09375
- w_down: bfloat16 [11008, 4096], P('tp', 'kv'), may hold values from -0.0546875 to 0.0546875
Outputs:
- layer_out: bfloat16 [2048, 4096], P(('kv', 'tp'))
Inputs may be any that keep to these rules, and one draw needn't show every extreme that they name: `cache_len`: every length is a multiple of 128; some sequence uses the whole cache.
All inputs are finite; a program needn't handle non-finite values.
Results may differ from a plain program's by a relative error of at most 0.019.
The roundings to bfloat16 on the way count: a program that leaves them out, or rounds other values in their place, can miss the bound.
Values may be sent and summed in bfloat16 or wider, within the bound.
A program may use at most 192 MiB of HBM per device.

v0:
```python
import math
import jax
import jax.numpy as jnp
from jax import lax
from jax.sharding import PartitionSpec as P

EPSILON = 1e-05
MASKED = -1e30


def rms_scale(values_in, gain_vector):
    widened = values_in.astype(jnp.float32)
    mean_square = jnp.mean(widened * widened, axis=-1, keepdims=True)
    return (widened * lax.rsqrt(mean_square + EPSILON) * gain_vector).astype(jnp.bfloat16)


def per_device(
    hidden_in, gain_attn, w_qkv, cache_kv, cache_len, w_out, gain_mlp, w_gate_up, w_down
):
    local_heads = w_qkv.shape[1]
    head_dim = w_qkv.shape[2] // 3
    own_rows = hidden_in.shape[0]
    block_input = lax.all_gather(hidden_in, "tp", axis=0, tiled=True)
    block_rows = block_input.shape[0]
    normed = rms_scale(block_input, gain_attn)
    flat_qkv = w_qkv.reshape(w_qkv.shape[0], local_heads * 3 * head_dim)
    packed = jnp.dot(normed, flat_qkv, preferred_element_type=jnp.float32).astype(jnp.bfloat16)
    packed = packed.reshape(block_rows, local_heads, 3 * head_dim)
    key_mine = packed[:, :, head_dim : 2 * head_dim]
    value_mine = packed[:, :, 2 * head_dim :]
    query_rows = lax.all_gather(packed[:, :, :head_dim], "kv", axis=0, tiled=True)
    seq_count = cache_kv.shape[0]
    span_len = query_rows.shape[0] // seq_count
    kv_index = lax.axis_index("kv")
    cache_rows = cache_kv.shape[1]
    cache_pos = kv_index * cache_rows + jnp.arange(cache_rows, dtype=jnp.int32)
    own_seq = (kv_index * block_rows + jnp.arange(block_rows, dtype=jnp.int32)) // span_len
    row_peaks, masses, accums = ([], [], [])
    for seq_id in range(seq_count):
        query_block = query_rows[seq_id * span_len : (seq_id + 1) * span_len]
        joined_key_rows = jnp.concatenate([cache_kv[seq_id, :, :, :head_dim], key_mine], axis=0)
        joined_value_rows = jnp.concatenate([cache_kv[seq_id, :, :, head_dim:], value_mine], axis=0)
        usable = jnp.concatenate([cache_pos < cache_len[seq_id], own_seq == seq_id])
        logit_scores = jnp.einsum(
            "qhd,khd->hqk", query_block, joined_key_rows, preferred_element_type=jnp.float32
        ) / math.sqrt(head_dim)
        logit_scores = jnp.where(usable[None, None, :], logit_scores, MASKED)
        row_peak = jnp.max(logit_scores, axis=2)
        raw_weights = jnp.where(
            usable[None, None, :], jnp.exp(logit_scores - row_peak[:, :, None]), 0.0
        )
        row_peaks.append(row_peak.T)
        masses.append(jnp.sum(raw_weights, axis=2).T)
        accums.append(
            jnp.einsum(
                "hqk,khd->qhd",
                raw_weights.astype(jnp.bfloat16),
                joined_value_rows,
                preferred_element_type=jnp.float32,
            )
        )
    peak_all = jnp.concatenate(row_peaks, axis=0)
    mass_all = jnp.concatenate(masses, axis=0)
    accum_all = jnp.concatenate(accums, axis=0)
    peak_set, mass_set, accum_set = (
        lax.all_to_all(peak_all[None], "kv", split_axis=1, concat_axis=0, tiled=True),
        lax.all_to_all(mass_all[None], "kv", split_axis=1, concat_axis=0, tiled=True),
        lax.all_to_all(accum_all[None], "kv", split_axis=1, concat_axis=0, tiled=True),
    )
    peak_best = jnp.max(peak_set, axis=0)
    scaling = jnp.exp(peak_set - peak_best[None])
    mass_own = jnp.sum(mass_set * scaling, axis=0)
    accum_own = jnp.sum(accum_set * scaling[..., None], axis=0)
    attended = (
        (accum_own / mass_own[..., None])
        .astype(jnp.bfloat16)
        .reshape(block_rows, local_heads * head_dim)
    )
    tp_index = lax.axis_index("tp")
    heads_sum = lax.psum(
        jnp.dot(attended, w_out, preferred_element_type=jnp.float32).astype(jnp.bfloat16), "tp"
    ).astype(jnp.float32)
    residual = block_input.astype(jnp.float32) + heads_sum
    mlp_in = rms_scale(residual, gain_mlp)
    residual_own = lax.dynamic_slice_in_dim(residual, tp_index * own_rows, own_rows, 0)
    gate_up = jnp.einsum(
        "td,dgf->tgf",
        mlp_in,
        lax.all_gather(w_gate_up, "kv", axis=0, tiled=True),
        preferred_element_type=jnp.float32,
    )
    activated = (jax.nn.silu(gate_up[:, 0, :]) * gate_up[:, 1, :]).astype(jnp.bfloat16)
    down_terms = jnp.dot(
        activated,
        lax.all_gather(w_down, "kv", axis=1, tiled=True),
        preferred_element_type=jnp.float32,
    )
    down_own = lax.psum_scatter(
        down_terms.astype(jnp.bfloat16), "tp", scatter_dimension=0, tiled=True
    ).astype(jnp.float32)
    return (residual_own + down_own).astype(jnp.bfloat16)


def solution(mesh):
    in_specs = (
        P(("kv", "tp"), None),
        P(),
        P(None, "tp", None),
        P(None, "kv", "tp", None),
        P(),
        P("tp", None),
        P(),
        P("kv", None, "tp"),
        P("tp", "kv"),
    )
    out_specs = P(("kv", "tp"), None)
    return jax.shard_map(
        per_device, mesh=mesh, in_specs=in_specs, out_specs=out_specs, check_vma=False
    )
```

profile of v0, /device:TPU:0, one launch (start us, length us, event | category | flops | bytes accessed | tf_op | source)
XLA Modules:
  0.0 827.3 jit_solution(16002876231132787441)
XLA Ops:
  7.3 12.4 %copy.51 = bf16[512,8,4,384]{3,1,2,0:T(8,128)(2,1)} copy(bf16[512,8,4,384]{3,2,1,0:T(4,128)(2,1)} %bitcast.50) | data formatting | bytes 25165824
  19.7 65.3 %all-gather.5.cloned.1.call-done = bf16[512,4096]{1,0:T(8,128)(2,1)} async-done(((bf16[64,4096]{1,0:T(8,128)(2,1)}), bf16[512,4096]{1,0:T(8,128)(2,1)}) %all-gather.5.cloned.1.call-update) | async-done | bytes 4194320 | tf_op jit(solution)/shard_map/all_gather | solution.py:23
  88.1 11.0 %fusion.24 = bf16[512,1536]{1,0:T(8,128)(2,1)S(1)} fusion(bf16[4096,1536]{1,0:T(8,128)(2,1)} %bitcast.51, bf16[512,4096]{1,0:T(8,128)(2,1)} %all-gather.5.cloned.1.call-done, f32[4096]{0:T(1024)S(1)} %copy-done.5, f32[512]{0:T(512)S(1)} %add_rsqrt_fusion.1), kind=kOutput, calls=%fused_computation.37 | convolution fusion | flops 6451625984 | bytes 18368512 | tf_op jit(solution)/shard_map/dot_general | solution.py:27
  100.9 6.4 fusion.61
  122.2 19.7 %fusion.1 = (f32[4,1024]{1,0:T(4,128)S(1)}, f32[4,1024,2560]{2,1,0:T(8,128)}) fusion(pred[2560]{0:T(1024)(128)(4,1)S(1)} %pad_add_fusion.1, bf16[512,4,128]{2,0,1:T(8,128)(2,1)S(1)} %copy.48, bf16[2048,4,128]{2,0,1:T(8,128)(2,1)} %get-tuple-element.26, bf16[2048,4,128]{2,0,1:T(8,128)(2,1)} %all-gather.7.cloned.1.call-done), kind=kOutput, calls=%fused_computation.5 | convolution fusion | flops 2721050624 | bytes 45632000 | tf_op jit(solution)/shard_map/qhd,khd->hqk/dot_general | solution.py:44
  141.8 19.2 %fusion.4 = f32[4,1024]{1,0:T(4,128)S(1)} fusion(f32[4,1024,2560]{2,1,0:T(8,128)} %get-tuple-element.19, f32[4,1024]{1,0:T(4,128)S(1)} %get-tuple-element.18, pred[2560]{0:T(1024)(128)(4,1)S(1)} %pad_add_fusion.1), kind=kLoop, calls=%fused_computation.8 | loop fusion | flops 52424704 | bytes 41978368 | tf_op jit(solution)/shard_map/reduce_sum | solution.py:53
  161.1 17.9 %fusion.38 = f32[1024,4,128]{0,2,1:T(8,128)} fusion(f32[4,1024,2560]{2,1,0:T(8,128)} %get-tuple-element.19, f32[4,1024]{1,0:T(4,128)S(1)} %get-tuple-element.18, pred[2560]{0:T(1024)(128)(4,1)S(1)} %pad_add_fusion.1, bf16[512,4,128]{0,2,1:T(8,128)(2,1)S(1)} %copy-done.3, bf16[2048,4,128]{0,2,1:T(8,128)(2,1)S(1)} %bitcast.59), kind=kOutput, calls=%fused_computation.51 | convolution fusion | flops 2742026240 | bytes 46680576 | tf_op jit(solution)/shard_map/hqk,khd->qhd/dot_general | solution.py:55
  178.9 19.0 %fusion = (f32[4,1024]{1,0:T(4,128)S(1)}, f32[4,1024,2560]{2,1,0:T(8,128)}) fusion(pred[2560]{0:T(1024)(128)(4,1)S(1)} %pad_add_fusion, bf16[512,4,128]{2,0,1:T(8,128)(2,1)S(1)} %copy.48, bf16[2048,4,128]{2,0,1:T(8,128)(2,1)S(1)} %get-tuple-element.27, bf16[2048,4,128]{2,0,1:T(8,128)(2,1)} %all-gather.7.cloned.1.call-done), kind=kOutput, calls=%fused_computation.4 | convolution fusion | flops 2721050624 | bytes 45632000 | tf_op jit(solution)/shard_map/qhd,khd->hqk/dot_general | solution.py:44
  198.0 19.2 %fusion.2 = f32[4,1024]{1,0:T(4,128)S(1)} fusion(f32[4,1024,2560]{2,1,0:T(8,128)} %get-tuple-element.21, f32[4,1024]{1,0:T(4,128)S(1)} %get-tuple-element.20, pred[2560]{0:T(1024)(128)(4,1)S(1)} %pad_add_fusion), kind=kLoop, calls=%fused_computation.6 | loop fusion | flops 52424704 | bytes 41978368 | tf_op jit(solution)/shard_map/reduce_sum | solution.py:53
  217.2 17.9 %fusion.35 = f32[1024,4,128]{0,2,1:T(8,128)} fusion(f32[4,1024,2560]{2,1,0:T(8,128)} %get-tuple-element.21, f32[4,1024]{1,0:T(4,128)S(1)} %get-tuple-element.20, pred[2560]{0:T(1024)(128)(4,1)S(1)} %pad_add_fusion, bf16[512,4,128]{0,2,1:T(8,128)(2,1)S(1)} %copy-done.3, bf16[2048,4,128]{0,2,1:T(8,128)(2,1)S(1)} %bitcast.58), kind=kOutput, calls=%fused_computation.50 | convolution fusion | flops 2742026240 | bytes 46680576 | tf_op jit(solution)/shard_map/hqk,khd->qhd/dot_general | solution.py:55
  236.1 9.5 %reduce.2 = f32[2048,4]{1,0:T(8,128)S(1)} reduce(f32[2048,1,4]{2,1,0:T(1,128)S(1)} %bitcast.54, f32[]{:T(128)} %broadcast.98), dimensions={1}, to_apply=%bitcast.41.reduce_sub_computation | reduce | bytes 65540
  250.6 9.3 %reduce = f32[2048,4]{1,0:T(8,128)S(1)} reduce(f32[2048,1,4]{2,1,0:T(1,128)S(1)} %bitcast.55, f32[]{:T(128)} %broadcast.98), dimensions={1}, to_apply=%bitcast.43.reduce_sub_computation | reduce | bytes 65540
  269.2 5.2 copy.37
  274.5 4.9 all-to-all-start
  285.5 42.0 %all-to-all-done = f32[1,2048,4,128]{3,2,0,1:T(4,128)} async-done(((f32[1,2048,4,128]{3,2,0,1:T(4,128)}), f32[1,2048,4,128]{3,2,0,1:T(4,128)}, u32[]{:S(2)}, u32[]{:S(2)}) %all-to-all-start) | async-done | bytes 4194336 | tf_op jit(solution)/shard_map/all_to_all | solution.py:68
  327.5 5.3 copy.41
  332.9 5.1 multiply_reduce_fusion.1
  344.1 155.1 %all-reduce.2.cloned.1.call-done = bf16[512,4096]{1,0:T(8,128)(2,1)} async-done(((bf16[512,4096]{1,0:T(8,128)(2,1)}), bf16[512,4096]{1,0:T(8,128)(2,1)}) %all-reduce.2.cloned.1.call-update) | async-done | bytes 4194320 | tf_op jit(solution)/shard_map/psum | solution.py:80
  499.2 9.2 %convert_add_fusion = (f32[512,4096]{1,0:T(8,128)}, f32[512]{0:T(512)S(1)}) fusion(bf16[512,4096]{1,0:T(8,128)(2,1)} %all-gather.5.cloned.1.call-done, bf16[512,4096]{1,0:T(8,128)(2,1)} %all-reduce.2.cloned.1.call-done), kind=kLoop, calls=%fused_computation.14 | loop fusion | flops 10485248 | bytes 16779264 | tf_op jit(solution)/shard_map/add | solution.py:83
  508.4 131.6 %all-gather.9.cloned.1.call-done = bf16[4096,2,1376]{0,2,1:T(8,128)(2,1)} async-done(((bf16[1024,2,1376]{0,2,1:T(8,128)(2,1)}), bf16[4096,2,1376]{0,2,1:T(8,128)(2,1)}) %all-gather.9.cloned.1.call-update) | async-done | bytes 22544400 | tf_op jit(solution)/shard_map/all_gather | solution.py:89
  639.9 20.5 %fusion.16 = f32[512,2,1376]{0,2,1:T(8,128)} fusion(bf16[4096,2,1376]{0,2,1:T(8,128)(2,1)} %all-gather.9.cloned.1.call-done, f32[4096]{0:T(1024)S(1)} %copy-done.6, f32[512]{0:T(512)S(1)} %add_rsqrt_fusion, bf16[512,4096]{1,0:T(8,128)(2,1)} %all-gather.5.cloned.1.call-done, bf16[512,4096]{1,0:T(8,128)(2,1)} %all-reduce.2.cloned.1.call-done), kind=kOutput, calls=%fused_computation.25 | convolution fusion | flops 11555307520 | bytes 36587520 | tf_op jit(solution)/shard_map/td,dgf->tgf/dot_general | solution.py:86
  660.4 55.6 %all-gather.11.cloned.1.call-done = bf16[1376,4096]{1,0:T(8,128)(2,1)} async-done(((bf16[1376,1024]{1,0:T(8,128)(2,1)}), bf16[1376,4096]{1,0:T(8,128)(2,1)}) %all-gather.11.cloned.1.call-update) | async-done | bytes 11272208 | tf_op jit(solution)/shard_map/all_gather | solution.py:95
  716.0 13.6 %convolution_convert_fusion = bf16[512,4096]{1,0:T(8,128)(2,1)} fusion(bf16[1376,4096]{1,0:T(8,128)(2,1)} %all-gather.11.cloned.1.call-done, f32[512,2,1376]{0,2,1:T(8,128)} %fusion.16), kind=kOutput, calls=%fused_computation.22 | convolution fusion | flops 5777686528 | bytes 21102592 | tf_op jit(solution)/shard_map/dot_general | solution.py:93
  729.6 88.4 %reduce-scatter.2.cloned.1.call-done = bf16[64,4096]{1,0:T(8,128)(2,1)} async-done(((bf16[512,4096]{1,0:T(8,128)(2,1)}), bf16[64,4096]{1,0:T(8,128)(2,1)}) %reduce-scatter.2.cloned.1.call-update) | async-done | bytes 524304 | tf_op jit(solution)/shard_map/reduce_scatter | solution.py:98
  (67 shorter events, 50.1 us)
Async XLA Ops:
  6.5 78.5 %all-gather.5.cloned.1.call-start = ((), (), s32[]{:S(2)}) async-start(), calls=%async_computation.4 | async-start | bytes 4718592 | tf_op jit(solution)/shard_map/all_gather | solution.py:23
  7.3 114.9 %all-gather.7.cloned.1.call-start = ((), (), s32[]{:S(2)}) async-start(), calls=%async_computation.5 | async-start | bytes 2621440 | tf_op jit(solution)/shard_map/all_gather | solution.py:31
  7.3 80.8 %copy-start.5 = (f32[4096]{0:T(1024)S(1)}, f32[4096]{0:T(1024)}, u32[]{:S(2)}) copy-start(f32[4096]{0:T(1024)} %param.10) | copy-start | bytes 49156
  107.4 7.1 copy-start.4
  141.8 19.2 %copy-start.2 = (bf16[1,2048,4,128]{1,3,2,0:T(8,128)(2,1)S(1)}, bf16[1,2048,4,128]{1,3,2,0:T(8,128)(2,1)}, u32[]{:S(2)}) copy-start(bf16[1,2048,4,128]{1,3,2,0:T(8,128)(2,1)} %copy.49) | copy-start | bytes 6291460
  141.8 19.2 %copy-start.3 = (bf16[512,4,128]{0,2,1:T(8,128)(2,1)S(1)}, bf16[512,4,128]{0,2,1:T(8,128)(2,1)}, u32[]{:S(2)}) copy-start(bf16[512,4,128]{0,2,1:T(8,128)(2,1)} %copy.45) | copy-start | bytes 1572868
  198.0 19.2 %copy-start.1 = (bf16[1,2048,4,128]{1,3,2,0:T(8,128)(2,1)S(1)}, bf16[1,2048,4,128]{1,3,2,0:T(8,128)(2,1)}, u32[]{:S(2)}) copy-start(bf16[1,2048,4,128]{1,3,2,0:T(8,128)(2,1)} %copy.44) | copy-start | bytes 6291460
  247.0 14.4 %all-to-all-start.1 = ((f32[4,1,2048]{2,1,0:T(1,128)}), f32[4,1,2048]{2,1,0:T(1,128)S(1)}, u32[]{:S(2)}, u32[]{:S(2)}) async-start(f32[4,1,2048]{2,1,0:T(1,128)} %reshape.59), calls=%async_computation.1 | async-start | bytes 65536 | tf_op jit(solution)/shard_map/all_to_all | solution.py:66
  261.3 13.2 %all-to-all-start.2 = ((f32[4,1,2048]{2,1,0:T(1,128)}), f32[4,1,2048]{2,1,0:T(1,128)S(1)}, u32[]{:S(2)}, u32[]{:S(2)}) async-start(f32[4,1,2048]{2,1,0:T(1,128)} %reshape.61), calls=%async_computation.2 | async-start | bytes 65536 | tf_op jit(solution)/shard_map/all_to_all | solution.py:67
  274.5 53.1 %all-to-all-start = ((f32[1,2048,4,128]{3,2,0,1:T(4,128)}), f32[1,2048,4,128]{3,2,0,1:T(4,128)}, u32[]{:S(2)}, u32[]{:S(2)}) async-start(f32[1,2048,4,128]{3,2,0,1:T(4,128)} %copy.37), calls=%async_computation | async-start | bytes 8388608 | tf_op jit(solution)/shard_map/all_to_all | solution.py:68
  279.3 219.8 %all-reduce.2.cloned.1.call-start = ((), (), s32[]{:S(2)}) async-start(), calls=%async_computation.6 | async-start | bytes 8388608 | tf_op jit(solution)/shard_map/psum | solution.py:80
  332.9 5.3 copy-start
  342.7 297.3 %all-gather.9.cloned.1.call-start = ((), (), s32[]{:S(2)}) async-start(), calls=%async_computation.7 | async-start | bytes 28180480 | tf_op jit(solution)/shard_map/all_gather | solution.py:89
  343.2 372.8 %all-gather.11.cloned.1.call-start = ((), (), s32[]{:S(2)}) async-start(), calls=%async_computation.8 | async-start | bytes 14090240 | tf_op jit(solution)/shard_map/all_gather | solution.py:95
  343.8 296.1 %copy-start.6 = (f32[4096]{0:T(1024)S(1)}, f32[4096]{0:T(1024)}, u32[]{:S(2)}) copy-start(f32[4096]{0:T(1024)} %param.15) | copy-start | bytes 49156
  343.8 474.2 %reduce-scatter.2.cloned.1.call-start = ((), (), s32[]{:S(2)}) async-start(), calls=%async_computation.9 | async-start | bytes 4718592 | tf_op jit(solution)/shard_map/reduce_scatter | solution.py:98
Sparse Core Ops, SparseCore 0:
  9.5 75.5 all-gather.4
  101.0 21.0 all-gather.6
  342.8 156.3 all-reduce.1
  500.6 139.2 all-gather.8
  641.3 74.6 all-gather.10
  729.7 88.2 reduce-scatter.1
where the time goes:
time: 835 us; the launch traced here: 827 us
  waiting for transfers between devices  540 us (65%)
  matrix products  124 us (15%)
  other arithmetic  84.6 us (10%)
  local copies, waits for them, and re-layouts  52.2 us (6%)
  between operations  13.9 us (2%)
  starting transfers between devices  12.2 us (1%)
    psum x1, waiting for transfers between devices, per_device(): lax.psum(jnp.dot(attended, w_out, preferred_element_type=jnp.float32).ast...  155 us
    all_gather x1, waiting for transfers between devices, per_device(): lax.all_gather(w_gate_up, 'kv', axis=0, tiled=True)  132 us
    reduce_scatter x1, waiting for transfers between devices, per_device(): lax.psum_scatter(down_terms.astype(jnp.bfloat16), 'tp', scatter_dimension...  88.4 us
    all_gather x1, waiting for transfers between devices, per_device(): block_input = lax.all_gather(hidden_in, 'tp', axis=0, tiled=True)  65.3 us
    all_gather x1, waiting for transfers between devices, per_device(): lax.all_gather(w_down, 'kv', axis=1, tiled=True)  55.6 us
    all_to_all x1, waiting for transfers between devices, per_device(): lax.all_to_all(accum_all[None], 'kv', split_axis=1, concat_axis=0, tiled=...  42 us
    dot_general x2, matrix products, per_device(): jnp.einsum('qhd,khd->hqk', query_block, joined_key_rows, preferred_elemen...  38.7 us
    reduce_sum x2, other arithmetic, per_device(): masses.append(jnp.sum(raw_weights, axis=2).T)  38.4 us
  transfers between devices with their start and end apart: 9, of which 7 were waited for; matrix products, arithmetic and copies ran while one was open for 11% of the time, Pallas kernels for 0%

commit v1 on v0

--- a/solution.py
+++ b/solution.py
@@ -6,6 +6,22 @@
 
 EPSILON = 1e-05
 MASKED = -1e30
+
+
+def ring_product(value, axis, dim, product):
+    peers, here, span = (lax.axis_size(axis), lax.axis_index(axis), value.shape[dim])
+    upward = [(i, (i + 1) % peers) for i in range(peers)]
+    left = [(i, (i - 1) % peers) for i in range(peers)]
+    halfway = peers // 2
+    from_left = from_right = value
+    total = product(value, here * span)
+    for step in range(1, halfway + 1):
+        from_left = lax.ppermute(from_left, axis, upward)
+        if step < peers - halfway:
+            from_right = lax.ppermute(from_right, axis, left)
+            total = total + product(from_right, (here + step) % peers * span)
+        total = total + product(from_left, (here - step) % peers * span)
+    return total
 
 
 def rms_scale(values_in, gain_vector):
@@ -83,11 +99,16 @@
     residual = block_input.astype(jnp.float32) + heads_sum
     mlp_in = rms_scale(residual, gain_mlp)
     residual_own = lax.dynamic_slice_in_dim(residual, tp_index * own_rows, own_rows, 0)
-    gate_up = jnp.einsum(
-        "td,dgf->tgf",
-        mlp_in,
-        lax.all_gather(w_gate_up, "kv", axis=0, tiled=True),
-        preferred_element_type=jnp.float32,
+    gate_up = ring_product(
+        w_gate_up,
+        "kv",
+        0,
+        lambda shard, offset: jnp.einsum(
+            "td,dgf->tgf",
+            lax.dynamic_slice_in_dim(mlp_in, offset, shard.shape[0], axis=1),
+            shard,
+            preferred_element_type=jnp.float32,
+        ),
     )
     activated = (jax.nn.silu(gate_up[:, 0, :]) * gate_up[:, 1, :]).astype(jnp.bfloat16)
     down_terms = jnp.dot(

time: 835 us -> 712 us (0.85)
  waiting for transfers between devices: 540 us -> 406 us
    ppermute x0 -> x3, waiting for transfers between devices: none -> 159 us  [the longest x2 159 us: ring_product(): from_left = lax.ppermute(from_left, axis, upward)]
    all_gather x1 -> x0, waiting for transfers between devices: 132 us -> none  [per_device(): lax.all_gather(w_gate_up, 'kv', axis=0, tiled=True)]
    psum x1, waiting for transfers between devices: 155 us -> 32.5 us  [per_device(): lax.psum(jnp.dot(attended, w_out, preferred_element_type=jnp.float32).ast...]
    all_gather x1, waiting for transfers between devices: 55.6 us -> 16.4 us  [per_device(): lax.all_gather(w_down, 'kv', axis=1, tiled=True)]
    dot_general x1 -> x4, matrix products: 20.5 us -> 28.6 us  [per_device(): jnp.einsum('td,dgf->tgf', lax.dynamic_slice_in_dim(mlp_in, offset, shard....]
    unnamed x25 -> x29, local copies, waits for them, and re-layouts: 28.1 us -> 28.1 us
  transfers between devices with their start and end apart: 9 -> 11, of which waited for: 7 -> 8; matrix products, arithmetic and copies ran while one was open for 11% -> 14% of each run, Pallas kernels for 0% -> 0%
where the time goes in v1:
time: 712 us; the launch traced here: 704 us
  waiting for transfers between devices  406 us (57%)
  matrix products  132 us (19%)
  other arithmetic  86.9 us (12%)
  local copies, waits for them, and re-layouts  52.3 us (7%)
  between operations  13.7 us (2%)
  starting transfers between devices  13.5 us (2%)
    ppermute x2, waiting for transfers between devices, ring_product(): from_left = lax.ppermute(from_left, axis, upward)  159 us
    reduce_scatter x1, waiting for transfers between devices, per_device(): lax.psum_scatter(down_terms.astype(jnp.bfloat16), 'tp', scatter_dimension...  88.9 us
    all_gather x1, waiting for transfers between devices, per_device(): block_input = lax.all_gather(hidden_in, 'tp', axis=0, tiled=True)  65.3 us
    all_to_all x1, waiting for transfers between devices, per_device(): lax.all_to_all(accum_all[None], 'kv', split_axis=1, concat_axis=0, tiled=...  42.3 us
    reduce_sum x2, other arithmetic, per_device(): masses.append(jnp.sum(raw_weights, axis=2).T)  38.4 us
    dot_general x2, matrix products, per_device(): jnp.einsum('qhd,khd->hqk', query_block, joined_key_rows, preferred_elemen...  38.4 us
    dot_general x2, matrix products, per_device(): jnp.einsum('hqk,khd->qhd', raw_weights.astype(jnp.bfloat16), joined_value...  35.8 us
    psum x1, waiting for transfers between devices, per_device(): lax.psum(jnp.dot(attended, w_out, preferred_element_type=jnp.float32).ast...  32.5 us
  transfers between devices with their start and end apart: 11, of which 8 were waited for; matrix products, arithmetic and copies ran while one was open for 14% of the time, Pallas kernels for 0%

profile of v1, /device:TPU:0, one launch (start us, length us, event | category | flops | bytes accessed | tf_op | source)
XLA Modules:
  0.0 704.0 jit_solution(4152850163955019507)
XLA Ops:
  7.3 12.4 %copy.51 = bf16[512,8,4,384]{3,1,2,0:T(8,128)(2,1)} copy(bf16[512,8,4,384]{3,2,1,0:T(4,128)(2,1)} %bitcast.62) | data formatting | bytes 25165824
  19.7 65.3 %all-gather.4.cloned.1.call-done = bf16[512,4096]{1,0:T(8,128)(2,1)} async-done(((bf16[64,4096]{1,0:T(8,128)(2,1)}), bf16[512,4096]{1,0:T(8,128)(2,1)}) %all-gather.4.cloned.1.call-update) | async-done | bytes 4194320 | tf_op jit(solution)/shard_map/all_gather | solution.py:39
  88.1 11.0 %fusion.19 = bf16[512,1536]{1,0:T(8,128)(2,1)S(1)} fusion(bf16[4096,1536]{1,0:T(8,128)(2,1)} %bitcast.63, bf16[512,4096]{1,0:T(8,128)(2,1)} %all-gather.4.cloned.1.call-done, f32[4096]{0:T(1024)S(1)} %copy-done.8, f32[512]{0:T(512)S(1)} %add_rsqrt_fusion.1), kind=kOutput, calls=%fused_computation.34 | convolution fusion | flops 6451625984 | bytes 18368512 | tf_op jit(solution)/shard_map/dot_general | solution.py:43
  100.9 6.4 fusion.71
  122.2 19.3 %fusion.1 = (f32[4,1024]{1,0:T(4,128)S(1)}, f32[4,1024,2560]{2,1,0:T(8,128)}) fusion(pred[2560]{0:T(1024)(128)(4,1)S(1)} %pad_add_fusion.1, bf16[512,4,128]{2,0,1:T(8,128)(2,1)S(1)} %copy.48, bf16[2048,4,128]{2,0,1:T(8,128)(2,1)} %get-tuple-element.26, bf16[2048,4,128]{2,0,1:T(8,128)(2,1)} %all-gather.6.cloned.1.call-done), kind=kOutput, calls=%fused_computation.5 | convolution fusion | flops 2721050624 | bytes 45632000 | tf_op jit(solution)/shard_map/qhd,khd->hqk/dot_general | solution.py:60
  141.5 19.2 %fusion.4 = f32[4,1024]{1,0:T(4,128)S(1)} fusion(f32[4,1024,2560]{2,1,0:T(8,128)} %get-tuple-element.19, f32[4,1024]{1,0:T(4,128)S(1)} %get-tuple-element.18, pred[2560]{0:T(1024)(128)(4,1)S(1)} %pad_add_fusion.1), kind=kLoop, calls=%fused_computation.8 | loop fusion | flops 52424704 | bytes 41978368 | tf_op jit(solution)/shard_map/reduce_sum | solution.py:69
  160.7 17.9 %fusion.33 = f32[1024,4,128]{0,2,1:T(8,128)} fusion(f32[4,1024,2560]{2,1,0:T(8,128)} %get-tuple-element.19, f32[4,1024]{1,0:T(4,128)S(1)} %get-tuple-element.18, pred[2560]{0:T(1024)(128)(4,1)S(1)} %pad_add_fusion.1, bf16[512,4,128]{0,2,1:T(8,128)(2,1)S(1)} %copy-done.5, bf16[2048,4,128]{0,2,1:T(8,128)(2,1)S(1)} %bitcast.71), kind=kOutput, calls=%fused_computation.48 | convolution fusion | flops 2742026240 | bytes 46680576 | tf_op jit(solution)/shard_map/hqk,khd->qhd/dot_general | solution.py:71
  178.6 19.1 %fusion = (f32[4,1024]{1,0:T(4,128)S(1)}, f32[4,1024,2560]{2,1,0:T(8,128)}) fusion(pred[2560]{0:T(1024)(128)(4,1)S(1)} %pad_add_fusion, bf16[512,4,128]{2,0,1:T(8,128)(2,1)S(1)} %copy.48, bf16[2048,4,128]{2,0,1:T(8,128)(2,1)S(1)} %get-tuple-element.27, bf16[2048,4,128]{2,0,1:T(8,128)(2,1)} %all-gather.6.cloned.1.call-done), kind=kOutput, calls=%fused_computation.4 | convolution fusion | flops 2721050624 | bytes 45632000 | tf_op jit(solution)/shard_map/qhd,khd->hqk/dot_general | solution.py:60
  197.7 19.2 %fusion.2 = f32[4,1024]{1,0:T(4,128)S(1)} fusion(f32[4,1024,2560]{2,1,0:T(8,128)} %get-tuple-element.21, f32[4,1024]{1,0:T(4,128)S(1)} %get-tuple-element.20, pred[2560]{0:T(1024)(128)(4,1)S(1)} %pad_add_fusion), kind=kLoop, calls=%fused_computation.6 | loop fusion | flops 52424704 | bytes 41978368 | tf_op jit(solution)/shard_map/reduce_sum | solution.py:69
  216.9 17.9 %fusion.30 = f32[1024,4,128]{0,2,1:T(8,128)} fusion(f32[4,1024,2560]{2,1,0:T(8,128)} %get-tuple-element.21, f32[4,1024]{1,0:T(4,128)S(1)} %get-tuple-element.20, pred[2560]{0:T(1024)(128)(4,1)S(1)} %pad_add_fusion, bf16[512,4,128]{0,2,1:T(8,128)(2,1)S(1)} %copy-done.5, bf16[2048,4,128]{0,2,1:T(8,128)(2,1)S(1)} %bitcast.70), kind=kOutput, calls=%fused_computation.47 | convolution fusion | flops 2742026240 | bytes 46680576 | tf_op jit(solution)/shard_map/hqk,khd->qhd/dot_general | solution.py:71
  235.7 9.7 %reduce.2 = f32[2048,4]{1,0:T(8,128)S(1)} reduce(f32[2048,1,4]{2,1,0:T(1,128)S(1)} %bitcast.66, f32[]{:T(128)} %broadcast.101), dimensions={1}, to_apply=%bitcast.50.reduce_sub_computation | reduce | bytes 65540
  250.5 9.3 %reduce = f32[2048,4]{1,0:T(8,128)S(1)} reduce(f32[2048,1,4]{2,1,0:T(1,128)S(1)} %bitcast.67, f32[]{:T(128)} %broadcast.101), dimensions={1}, to_apply=%bitcast.52.reduce_sub_computation | reduce | bytes 65540
  285.1 42.3 %all-to-all-done = f32[1,2048,4,128]{3,2,0,1:T(4,128)} async-done(((f32[1,2048,4,128]{3,2,0,1:T(4,128)}), f32[1,2048,4,128]{3,2,0,1:T(4,128)}, u32[]{:S(2)}, u32[]{:S(2)}) %all-to-all-start) | async-done | bytes 4194336 | tf_op jit(solution)/shard_map/all_to_all | solution.py:84
  327.4 5.3 copy.41
  344.9 121.6 %collective-permute-done.1 = bf16[1024,2,1376]{0,2,1:T(8,128)(2,1)} collective-permute-done((bf16[1024,2,1376]{0,2,1:T(8,128)(2,1)}, bf16[1024,2,1376]{0,2,1:T(8,128)(2,1)}, u32[]{:S(2)}, u32[]{:S(2)}) %collective-permute-start.1) | collective-permute-done | bytes 5636128 | tf_op jit(solution)/shard_map/ppermute | solution.py:19
  466.5 32.5 %all-reduce.2.cloned.1.call-done = bf16[512,4096]{1,0:T(8,128)(2,1)} async-done(((bf16[512,4096]{1,0:T(8,128)(2,1)}), bf16[512,4096]{1,0:T(8,128)(2,1)}) %all-reduce.2.cloned.1.call-update) | async-done | bytes 4194320 | tf_op jit(solution)/shard_map/psum | solution.py:96
  499.0 8.9 %convert_add_fusion = (f32[512,4096]{1,0:T(8,128)}, f32[512]{0:T(512)S(1)}) fusion(bf16[512,4096]{1,0:T(8,128)(2,1)} %all-gather.4.cloned.1.call-done, bf16[512,4096]{1,0:T(8,128)(2,1)} %all-reduce.2.cloned.1.call-done), kind=kLoop, calls=%fused_computation.14 | loop fusion | flops 10485248 | bytes 16779264 | tf_op jit(solution)/shard_map/add | solution.py:99
  510.4 6.3 fusion.45
  522.0 7.7 %fusion.43 = f32[512,2,1376]{0,2,1:T(8,128)} fusion(bf16[1024,2,1376]{0,2,1:T(8,128)(2,1)} %collective-permute-done, bf16[512,4096]{1,0:T(8,128)(2,1)S(1)} %multiply_convert_fusion, s32[]{:T(128)S(6)} %select_n.56), kind=kOutput, calls=%fused_computation.55 | convolution fusion | flops 2885681152 | bytes 12320772 | tf_op jit(solution)/shard_map/td,dgf->tgf/dot_general | solution.py:106
  529.7 37.0 %collective-permute-done.2 = bf16[1024,2,1376]{0,2,1:T(8,128)(2,1)} collective-permute-done((bf16[1024,2,1376]{0,2,1:T(8,128)(2,1)}, bf16[1024,2,1376]{0,2,1:T(8,128)(2,1)}, u32[]{:S(2)}, u32[]{:S(2)}) %collective-permute-start.2) | collective-permute-done | bytes 5636128 | tf_op jit(solution)/shard_map/ppermute | solution.py:19
  566.7 9.4 %add_add_fusion = f32[512,2,1376]{0,2,1:T(8,128)} fusion(f32[512,2,1376]{0,2,1:T(8,128)S(1)} %fusion.41, f32[512,2,1376]{0,2,1:T(8,128)S(1)} %fusion.45, f32[512,2,1376]{0,2,1:T(8,128)} %fusion.43, bf16[1024,2,1376]{0,2,1:T(8,128)(2,1)} %collective-permute-done.2, bf16[512,4096]{1,0:T(8,128)(2,1)S(1)} %multiply_convert_fusion, s32[]{:T(128)S(6)} %select_n.60), kind=kOutput, calls=%fused_computation.24 | convolution fusion | flops 2889908224 | bytes 29229060 | tf_op jit(solution)/shard_map/td,dgf->tgf/dot_general | solution.py:106
  576.1 16.4 %all-gather.8.cloned.1.call-done = bf16[1376,4096]{1,0:T(8,128)(2,1)} async-done(((bf16[1376,1024]{1,0:T(8,128)(2,1)}), bf16[1376,4096]{1,0:T(8,128)(2,1)}) %all-gather.8.cloned.1.call-update) | async-done | bytes 11272208 | tf_op jit(solution)/shard_map/all_gather | solution.py:116
  592.4 13.7 %convolution_convert_fusion = bf16[512,4096]{1,0:T(8,128)(2,1)} fusion(bf16[1376,4096]{1,0:T(8,128)(2,1)} %all-gather.8.cloned.1.call-done, f32[512,2,1376]{0,2,1:T(8,128)} %add_add_fusion), kind=kOutput, calls=%fused_computation.22 | convolution fusion | flops 5777686528 | bytes 21102592 | tf_op jit(solution)/shard_map/dot_general | solution.py:114
  606.1 88.9 %reduce-scatter.2.cloned.1.call-done = bf16[64,4096]{1,0:T(8,128)(2,1)} async-done(((bf16[512,4096]{1,0:T(8,128)(2,1)}), bf16[64,4096]{1,0:T(8,128)(2,1)}) %reduce-scatter.2.cloned.1.call-update) | async-done | bytes 524304 | tf_op jit(solution)/shard_map/reduce_scatter | solution.py:119
  (78 shorter events, 73.7 us)
Async XLA Ops:
  6.5 78.5 %all-gather.4.cloned.1.call-start = ((), (), s32[]{:S(2)}) async-start(), calls=%async_computation.4 | async-start | bytes 4718592 | tf_op jit(solution)/shard_map/all_gather | solution.py:39
  7.3 114.9 %all-gather.6.cloned.1.call-start = ((), (), s32[]{:S(2)}) async-start(), calls=%async_computation.5 | async-start | bytes 2621440 | tf_op jit(solution)/shard_map/all_gather | solution.py:47
  7.3 80.8 %copy-start.8 = (f32[4096]{0:T(1024)S(1)}, f32[4096]{0:T(1024)}, u32[]{:S(2)}) copy-start(f32[4096]{0:T(1024)} %param.10) | copy-start | bytes 49156
  107.4 7.1 %copy-start.7 = (s32[2]{0:T(128)S(1)}, s32[2]{0:T(128)}, u32[]{:S(2)}) copy-start(s32[2]{0:T(128)} %param.13) | copy-start | bytes 28
  141.5 19.2 %copy-start.4 = (bf16[1,2048,4,128]{1,3,2,0:T(8,128)(2,1)S(1)}, bf16[1,2048,4,128]{1,3,2,0:T(8,128)(2,1)}, u32[]{:S(2)}) copy-start(bf16[1,2048,4,128]{1,3,2,0:T(8,128)(2,1)} %copy.49) | copy-start | bytes 6291460
  141.5 19.2 %copy-start.5 = (bf16[512,4,128]{0,2,1:T(8,128)(2,1)S(1)}, bf16[512,4,128]{0,2,1:T(8,128)(2,1)}, u32[]{:S(2)}) copy-start(bf16[512,4,128]{0,2,1:T(8,128)(2,1)} %copy.45) | copy-start | bytes 1572868
  197.7 19.2 %copy-start.3 = (bf16[1,2048,4,128]{1,3,2,0:T(8,128)(2,1)S(1)}, bf16[1,2048,4,128]{1,3,2,0:T(8,128)(2,1)}, u32[]{:S(2)}) copy-start(bf16[1,2048,4,128]{1,3,2,0:T(8,128)(2,1)} %copy.44) | copy-start | bytes 6291460
  246.8 14.3 %all-to-all-start.1 = ((f32[4,1,2048]{2,1,0:T(1,128)}), f32[4,1,2048]{2,1,0:T(1,128)S(1)}, u32[]{:S(2)}, u32[]{:S(2)}) async-start(f32[4,1,2048]{2,1,0:T(1,128)} %reshape.62), calls=%async_computation.1 | async-start | bytes 65536 | tf_op jit(solution)/shard_map/all_to_all | solution.py:82
  261.2 13.2 %all-to-all-start.2 = ((f32[4,1,2048]{2,1,0:T(1,128)}), f32[4,1,2048]{2,1,0:T(1,128)S(1)}, u32[]{:S(2)}, u32[]{:S(2)}) async-start(f32[4,1,2048]{2,1,0:T(1,128)} %reshape.64), calls=%async_computation.2 | async-start | bytes 65536 | tf_op jit(solution)/shard_map/all_to_all | solution.py:83
  274.3 53.1 %all-to-all-start = ((f32[1,2048,4,128]{3,2,0,1:T(4,128)}), f32[1,2048,4,128]{3,2,0,1:T(4,128)}, u32[]{:S(2)}, u32[]{:S(2)}) async-start(f32[1,2048,4,128]{3,2,0,1:T(4,128)} %copy.37), calls=%async_computation | async-start | bytes 8388608 | tf_op jit(solution)/shard_map/all_to_all | solution.py:84
  279.2 219.9 %all-reduce.2.cloned.1.call-start = ((), (), s32[]{:S(2)}) async-start(), calls=%async_computation.6 | async-start | bytes 8388608 | tf_op jit(solution)/shard_map/psum | solution.py:96
  332.7 5.3 copy-start.2
  342.5 249.9 %all-gather.8.cloned.1.call-start = ((), (), s32[]{:S(2)}) async-start(), calls=%async_computation.7 | async-start | bytes 14090240 | tf_op jit(solution)/shard_map/all_gather | solution.py:116
  343.1 351.9 %reduce-scatter.2.cloned.1.call-start = ((), (), s32[]{:S(2)}) async-start(), calls=%async_computation.8 | async-start | bytes 4718592 | tf_op jit(solution)/shard_map/reduce_scatter | solution.py:119
  343.1 123.4 %collective-permute-start.1 = (bf16[1024,2,1376]{0,2,1:T(8,128)(2,1)}, bf16[1024,2,1376]{0,2,1:T(8,128)(2,1)}, u32[]{:S(2)}, u32[]{:S(2)}) collective-permute-start(bf16[1024,2,1376]{0,2,1:T(8,128)(2,1)} %param.16), channel_id=1, source_target_pairs={{0,1},{1,2},{2,3},{3,0},{4,5},{5,6},{6,7},{7,4},{8,9},{9,10},{10,1... | collective-permute-start | bytes 16908296 | tf_op jit(solution)/shard_map/ppermute | solution.py:19
  343.2 178.8 %collective-permute-start = (bf16[1024,2,1376]{0,2,1:T(8,128)(2,1)}, bf16[1024,2,1376]{0,2,1:T(8,128)(2,1)}, u32[]{:S(2)}, u32[]{:S(2)}) collective-permute-start(bf16[1024,2,1376]{0,2,1:T(8,128)(2,1)} %param.16), channel_id=1, source_target_pairs={{0,3},{1,0},{2,1},{3,2},{4,7},{5,4},{6,5},{7,6},{8,11},{9,8},{10,9... | collective-permute-start | bytes 16908296 | tf_op jit(solution)/shard_map/ppermute | solution.py:21
  466.5 100.2 %collective-permute-start.2 = (bf16[1024,2,1376]{0,2,1:T(8,128)(2,1)}, bf16[1024,2,1376]{0,2,1:T(8,128)(2,1)}, u32[]{:S(2)}, u32[]{:S(2)}) collective-permute-start(bf16[1024,2,1376]{0,2,1:T(8,128)(2,1)} %collective-permute-done.1), channel_id=1, source_target_pairs={{0,1},{1,2},{2,3},{3,0},{4,5},{5,6},{6,7},{7,4},{8,9},{9,10},{10,1... | collective-permute-start | bytes 16908296 | tf_op jit(solution)/shard_map/ppermute | solution.py:19
  466.5 41.5 %copy-start.6 = (f32[4096]{0:T(1024)S(1)}, f32[4096]{0:T(1024)}, u32[]{:S(2)}) copy-start(f32[4096]{0:T(1024)} %param.15) | copy-start | bytes 49156
  499.0 9.0 %copy-start = (bf16[512,4096]{1,0:T(8,128)(2,1)S(1)}, bf16[512,4096]{1,0:T(8,128)(2,1)}, u32[]{:S(2)}) copy-start(bf16[512,4096]{1,0:T(8,128)(2,1)} %all-gather.4.cloned.1.call-done) | copy-start | bytes 12582916
  499.0 9.0 %copy-start.1 = (bf16[512,4096]{1,0:T(8,128)(2,1)S(1)}, bf16[512,4096]{1,0:T(8,128)(2,1)}, u32[]{:S(2)}) copy-start(bf16[512,4096]{1,0:T(8,128)(2,1)} %all-reduce.2.cloned.1.call-done) | copy-start | bytes 12582916
Sparse Core Ops, SparseCore 0:
  9.5 75.5 all-gather.3
  101.0 21.0 all-gather.5
  342.6 156.3 all-reduce.1
  500.5 91.9 all-gather.7
  606.2 88.7 reduce-scatter.1
